TPU v7x, 256 devices: a whole 4x4x8 slice. The times are simulated.
256 devices in a mesh: date: 16 (over z, core), book: 16 (over x, y).
Axes of the slice: x: 4, y: 4, z: 8, core: 2. Of those that a mesh axis runs over, the one named last changes fastest.
Arguments:
- shocks: bfloat16 [32, 512, 8192], P('date', None, 'book'), may hold values from -6 to 6
- persistence: float32 [8192], P('book'), may hold values from 0.5 to 1
- volatility: float32 [8192], P('book'), may hold values from 0.05 to 0.4
- base_rate: float32 [8192], P('book'), may hold values from 0 to 1
- cashflows: bfloat16 [65536, 512], P('book'), may hold values from -0.0625 to 0.0625
- block_owner: int32 [256, 1], P('book'), may hold values from 0 to 15; in each aligned block of 16 rows (0 to 15, 16 to 31, ...) at most 2 rows name the same one
- trade_set: int32 [65536], P('book'), may hold values from 0 to 511
- threshold: float32 [512], P('book'), may hold values from 0.1 to 1
- margin_lag: int32 [512], P('book'), may hold values from 1 to 2
Outputs:
- net_value: float32 [32, 512, 512], P('date', None, 'book')
- expected_exposure: float32 [32, 512], P('date', 'book')
Inputs may be any that keep to these rules, and one draw needn't show every extreme that they name: `block_owner`: among the blocks of one index of book, no value is named by more than 2 blocks.
All inputs are finite; a program needn't handle non-finite values.
Results may differ from a plain program's by a relative error of at most 0.0039.
Values may be sent and summed in bfloat16 or wider, within the bound.
A program may use at most 128 MiB of HBM per device.

v0:
```python
import jax
import jax.numpy as jnp
from jax import lax
from jax.sharding import PartitionSpec as P

SETS = 512


def prefix(array, axis, combine, identity):
    devices, here = (lax.axis_size(axis), lax.axis_index(axis))
    everything = jax.tree.map(lambda part: lax.all_gather(part, axis), array)
    start = jax.tree.map(
        lambda part, zero: jnp.broadcast_to(jnp.asarray(zero, part.dtype), part.shape),
        array,
        identity,
    )

    def hop(k, before):
        reached = k < here
        new = combine(before, jax.tree.map(lambda part: part[k], everything))
        return jax.tree.map(lambda a, b: jnp.where(reached, a, b), new, before)

    return lax.fori_loop(0, devices, hop, start)


def split_up(array, dim, devices):
    before, after = (array.shape[:dim], array.shape[dim + 1 :])
    return jnp.moveaxis(array.reshape(*before, devices, -1, *after), dim, 0)


def sent_and_summed(array, axis, dim):
    blocks = split_up(array, dim, lax.axis_size(axis))
    arrived = lax.all_to_all(blocks, axis, split_axis=0, concat_axis=0, tiled=True)
    return arrived.sum(axis=0)


def shifted(block, axis, distance):
    devices = range(lax.axis_size(axis))
    route = [(i - distance, i) for i in devices if i - distance in devices]
    return lax.ppermute(block, axis, route)


def combine(earlier, later):
    return (earlier[0] * later[0], later[0] * earlier[1] + later[1])


def on_device(
    shocks,
    persistence,
    volatility,
    base_rate,
    cashflows,
    block_owner,
    trade_set,
    threshold,
    margin_lag,
):
    dates_here = shocks.shape[0]
    paths = shocks.shape[1]
    width = shocks.shape[2]
    blocks = block_owner.shape[0]
    block_rows = cashflows.shape[0] // blocks
    rows = dates_here * paths
    books = lax.axis_size("book")
    driven = volatility * shocks.astype(jnp.float32)
    carried = jnp.zeros((paths, width), jnp.float32)
    for step in range(dates_here):
        carried = persistence * carried + driven[step]
    factor = persistence**dates_here
    identity = (jnp.ones_like(persistence), jnp.zeros((paths, width), jnp.float32))
    _, state = prefix((factor, carried), "date", combine, identity)
    levels = []
    for step in range(dates_here):
        state = persistence * state + driven[step]
        levels.append(state)
    level = jnp.stack(levels, 0)
    discount = jnp.exp(-(base_rate + level)).astype(jnp.bfloat16).reshape(rows, width)
    owners = block_owner[:, 0]
    labels = jnp.arange(SETS, dtype=jnp.int32)
    most = max(2, 2 * blocks // books)
    order = jnp.arange(blocks, dtype=jnp.int32)
    before = (owners[:, None] == owners[None, :]) & (order[:, None] > order[None, :])
    rank = jnp.sum(before.astype(jnp.int32), axis=1)
    slot = owners * most + rank
    place = slot[:, None] == jnp.arange(books * most, dtype=jnp.int32)[None, :]
    packed = jnp.einsum(
        "bs,bx->sx",
        place.astype(jnp.bfloat16),
        cashflows.reshape(blocks, block_rows * width),
        preferred_element_type=jnp.float32,
    )
    packed = packed.astype(jnp.bfloat16).reshape(books, most, block_rows, width)
    set_rows = trade_set.reshape(blocks, block_rows) + 1
    slot_sets = jnp.sum(jnp.where(place[:, :, None], set_rows[:, None, :], 0), axis=0) - 1
    slot_sets = slot_sets.reshape(books, most, block_rows)
    arrived, arrived_sets = (
        lax.all_to_all(packed, "book", split_axis=0, concat_axis=0, tiled=True),
        lax.all_to_all(slot_sets, "book", split_axis=0, concat_axis=0, tiled=True),
    )
    price = jnp.einsum(
        "rk,tk->rt", discount, arrived.reshape(-1, width), preferred_element_type=jnp.float32
    )
    price = price.astype(jnp.bfloat16)
    onehot = (arrived_sets.reshape(-1)[:, None] == labels[None, :]).astype(jnp.bfloat16)
    partial_sets = jnp.dot(price, onehot, preferred_element_type=jnp.float32).reshape(
        dates_here, paths, SETS
    )
    net_value = sent_and_summed(partial_sets, "book", 2)
    earlier = shifted(net_value, "date", 1)
    joined = jnp.concatenate([earlier, net_value], 0)
    collateral = jnp.zeros_like(net_value)
    for lag in range(1, dates_here + 1):
        collateral = jnp.where(
            margin_lag[None, None, :] == lag,
            joined[dates_here - lag : 2 * dates_here - lag],
            collateral,
        )
    exposure = jnp.maximum(net_value - collateral - threshold[None, None, :], 0.0)
    return (net_value, jnp.mean(exposure, axis=1))


def solution(mesh):
    return jax.shard_map(
        on_device,
        mesh=mesh,
        in_specs=(
            P("date", None, "book"),
            P("book"),
            P("book"),
            P("book"),
            P("book", None),
            P("book", None),
            P("book"),
            P("book"),
            P("book"),
        ),
        out_specs=(P("date", None, "book"), P("date", "book")),
        check_vma=False,
    )
```

profile of v0, /device:TPU:57, one launch (start us, length us, event | category | flops | bytes accessed | tf_op | source)
XLA Modules:
  0.0 275.3 jit_solution(5810079417902505108)
XLA Ops:
  12.5 6.6 %all-to-all-start.1 = ((s32[16,2,256]{2,1,0:T(2,128)}), s32[16,2,256]{2,1,0:T(2,128)S(1)}, u32[]{:S(2)}, u32[]{:S(2)}) async-start(s32[16,2,256]{2,1,0:T(2,128)} %sub.18), calls=%async_computation.1 | async-start | bytes 65536 | tf_op jit(solution)/shard_map/all_to_all | solution.py:98
  19.1 4.8 %reshape.94 = bf16[16,131072]{1,0:T(8,128)(2,1)} reshape(bf16[4096,512]{1,0:T(8,128)(2,1)} %param.15) | data formatting | bytes 8388608 | tf_op jit(solution)/shard_map/reshape | solution.py:89
  23.9 8.3 %convolution_convert_fusion = bf16[32,131072]{1,0:T(8,128)(2,1)} fusion(bf16[16,131072]{1,0:T(8,128)(2,1)} %reshape.94, s32[16]{0:T(128)S(1)} %fusion.13), kind=kOutput, calls=%fused_computation.3 | convolution fusion | flops 138412544 | bytes 12582976 | tf_op jit(solution)/shard_map/bs,bx->sx/dot_general | solution.py:86
  32.2 10.0 %copy.22 = bf16[4,8,256,512]{3,2,1,0:T(8,128)(2,1)} copy(bf16[4,8,256,512]{3,1,2,0:T(8,128)(2,1)} %bitcast.49) | data formatting | bytes 16777216
  42.2 6.7 %all-to-all-start = ((bf16[16,2,256,512]{3,2,1,0:T(8,128)(2,1)}), bf16[16,2,256,512]{3,2,1,0:T(8,128)(2,1)}, u32[]{:S(2)}, u32[]{:S(2)}) async-start(bf16[16,2,256,512]{3,2,1,0:T(8,128)(2,1)} %bitcast.48), calls=%async_computation | async-start | bytes 16777216 | tf_op jit(solution)/shard_map/all_to_all | solution.py:97
  48.9 19.9 %all-gather.1 = f32[16,1,512]{2,1,0:T(1,128)S(1)} all-gather(f32[1,1,512]{2,1,0:T(1,128)S(1)} %bitcast.56), channel_id=2, replica_groups=mesh['date'=16,'book'=16] {'date'}, dimensions={0}, use_global_device_ids=true | all-gather | bytes 34816 | tf_op jit(solution)/shard_map/all_gather | solution.py:11
  68.9 38.9 %all-gather.4.cloned.1.call-done = f32[16,512,512]{2,1,0:T(8,128)} async-done(((f32[1,512,512]{2,1,0:T(8,128)}), f32[16,512,512]{2,1,0:T(8,128)}) %all-gather.4.cloned.1.call-update) | async-done | bytes 16777232 | tf_op jit(solution)/shard_map/all_gather | solution.py:11
  107.8 34.8 %while.14 = (s32[]{:T(128)}, f32[512,512]{1,0:T(8,128)S(1)}, s32[]{:T(128)}, f32[16,512]{1,0:T(8,128)S(1)}, f32[16,512,512]{2,1,0:T(8,128)}, /*index=5*/s32[]{:T(128)}, s32[]{:T(128)}) while((s32[]{:T(128)}, f32[512,512]{1,0:T(8,128)S(1)}, s32[]{:T(128)}, f32[16,512]{1,0:T(8,128)S(1)}, f32[16,512,512]{2,1,0:T(8,128)}, ...), condition=%wide.region_1.2_spmd.clone, body=%wide.region_0.1_spmd.clone.sunk | while | flops 1048580 | bytes 3151977 | solution.py:23
  107.8 2.1 fusion.20
  110.0 2.1 fusion.20
  112.2 2.1 fusion.20
  114.4 2.1 fusion.20
  116.5 2.1 fusion.20
  118.7 2.1 fusion.20
  120.9 2.1 fusion.20
  123.1 2.1 fusion.20
  125.2 2.1 fusion.20
  127.4 2.1 fusion.20
  143.6 32.1 %all-to-all-done = bf16[16,2,256,512]{3,2,1,0:T(8,128)(2,1)} async-done(((bf16[16,2,256,512]{3,2,1,0:T(8,128)(2,1)}), bf16[16,2,256,512]{3,2,1,0:T(8,128)(2,1)}, u32[]{:S(2)}, u32[]{:S(2)}) %all-to-all-start) | async-done | bytes 8388640 | tf_op jit(solution)/shard_map/all_to_all | solution.py:97
  175.7 15.1 %fusion.14 = bf16[1024,8192]{1,0:T(8,128)(2,1)} fusion(bf16[1024,512]{1,0:T(8,128)(2,1)S(1)} %bitcast.51, bf16[8192,512]{1,0:T(8,128)(2,1)} %bitcast.9), kind=kOutput, calls=%fused_computation.37 | convolution fusion | flops 8589934592 | bytes 26214400 | tf_op jit(solution)/shard_map/rk,tk->rt/dot_general | solution.py:100
  190.9 13.6 %fusion.1 = f32[1024,512]{0,1:T(8,128)S(1)} fusion(bf16[1024,8192]{1,0:T(8,128)(2,1)} %fusion.14, s32[8192]{0:T(1024)S(1)} %bitcast.55), kind=kOutput, calls=%fused_computation.5 | convolution fusion | flops 8594128896 | bytes 18907136 | tf_op jit(solution)/shard_map/dot_general | solution.py:105
  204.4 2.8 %reshape_reshape.3 = f32[2,512,16,32]{1,0,3,2:T(2,128)} reshape(f32[1024,512]{0,1:T(8,128)S(1)} %fusion.1) | data formatting | bytes 4194304 | tf_op jit(solution)/shard_map/reshape;reshape | solution.py:28
  207.3 41.2 %all_to_all.15 = f32[16,2,512,32]{2,1,3,0:T(2,128)S(1)} all-to-all(f32[16,2,512,32]{2,1,3,0:T(2,128)} %bitcast.50), channel_id=1, replica_groups=mesh['date'=16,'book'=16] {'book'}, dimensions={0} | all-to-all | bytes 4194304 | tf_op jit(solution)/shard_map/all_to_all | solution.py:33
  249.4 16.1 %collective-permute-start = (f32[2,512,32]{1,0,2:T(2,128)S(1)}, f32[2,512,32]{1,0,2:T(2,128)S(1)}, u32[]{:S(2)}, u32[]{:S(2)}) collective-permute-start(f32[2,512,32]{1,0,2:T(2,128)S(1)} %reduce_sum.41), channel_id=1, source_target_pairs={{0,16},{16,32},{32,48},{48,64},{64,80},{80,96},{96,112},{112,128},... | collective-permute-start | bytes 393224 | tf_op jit(solution)/shard_map/ppermute | solution.py:40
  (60 shorter events, 22.9 us)
Async XLA Ops:
  7.2 4.2 %copy-start.1 = (s32[4096]{0:T(1024)S(1)}, s32[4096]{0:T(1024)}, u32[]{:S(2)}) copy-start(s32[4096]{0:T(1024)} %param.17) | copy-start | bytes 49156
  7.2 4.2 %copy-start.4 = (s32[16,1]{0,1:T(1,128)S(1)}, s32[16,1]{0,1:T(1,128)}, u32[]{:S(2)}) copy-start(s32[16,1]{0,1:T(1,128)} %param.16) | copy-start | bytes 196
  7.2 100.6 %all-gather.4.cloned.1.call-start = ((), (), s32[]{:S(2)}) async-start(), calls=%async_computation.3 | async-start | bytes 17825792 | tf_op jit(solution)/shard_map/all_gather | solution.py:11
  12.5 29.8 %all-to-all-start.1 = ((s32[16,2,256]{2,1,0:T(2,128)}), s32[16,2,256]{2,1,0:T(2,128)S(1)}, u32[]{:S(2)}, u32[]{:S(2)}) async-start(s32[16,2,256]{2,1,0:T(2,128)} %sub.18), calls=%async_computation.1 | async-start | bytes 65536 | tf_op jit(solution)/shard_map/all_to_all | solution.py:98
  42.2 133.5 %all-to-all-start = ((bf16[16,2,256,512]{3,2,1,0:T(8,128)(2,1)}), bf16[16,2,256,512]{3,2,1,0:T(8,128)(2,1)}, u32[]{:S(2)}, u32[]{:S(2)}) async-start(bf16[16,2,256,512]{3,2,1,0:T(8,128)(2,1)} %bitcast.48), calls=%async_computation | async-start | bytes 16777216 | tf_op jit(solution)/shard_map/all_to_all | solution.py:97
  107.8 34.9 %copy-start = (f32[512]{0:T(512)S(1)}, f32[512]{0:T(512)}, u32[]{:S(2)}) copy-start(f32[512]{0:T(512)} %param.12) | copy-start | bytes 6148
  142.6 0.7 copy-start.2
  207.3 58.2 %copy-start.5 = (s32[32]{0:T(128)S(1)}, s32[32]{0:T(128)}, u32[]{:S(2)}) copy-start(s32[32]{0:T(128)} %param.19) | copy-start | bytes 388
  207.3 60.1 %copy-start.3 = (f32[32]{0:T(128)S(1)}, f32[32]{0:T(128)}, u32[]{:S(2)}) copy-start(f32[32]{0:T(128)} %param.18) | copy-start | bytes 388
  249.4 18.1 %collective-permute-start = (f32[2,512,32]{1,0,2:T(2,128)S(1)}, f32[2,512,32]{1,0,2:T(2,128)S(1)}, u32[]{:S(2)}, u32[]{:S(2)}) collective-permute-start(f32[2,512,32]{1,0,2:T(2,128)S(1)} %reduce_sum.41), channel_id=1, source_target_pairs={{0,16},{16,32},{32,48},{48,64},{64,80},{80,96},{96,112},{112,128},... | collective-permute-start | bytes 393224 | tf_op jit(solution)/shard_map/ppermute | solution.py:40
Sparse Core Ops, SparseCore 0:
  11.5 96.2 all-gather.3
where the time goes:
time: 280 us; the launch traced here: 275 us
  waiting for transfers between devices  72.3 us (26%)
  blocking collectives  61.2 us (22%)
  other arithmetic  40.6 us (14%)
  matrix products  37 us (13%)
  starting transfers between devices  29.5 us (11%)
  local copies, waits for them, and re-layouts  20.1 us (7%)
  between operations  14.2 us (5%)
    all_to_all x1, blocking collectives, sent_and_summed(): lax.all_to_all(blocks, axis, split_axis=0, concat_axis=0, tiled=True)  41.2 us
    all_gather x1, waiting for transfers between devices, prefix(): everything = jax.tree.map(lambda part: lax.all_gather(part, axis), array)  38.9 us
    select_n x16, other arithmetic, hop(): return jax.tree.map(lambda a, b: jnp.where(reached, a, b), new, before)  34.2 us
    all_to_all x1, waiting for transfers between devices, on_device(): lax.all_to_all(packed, 'book', split_axis=0, concat_axis=0, tiled=True)  32.1 us
    all_gather x1, blocking collectives, prefix(): everything = jax.tree.map(lambda part: lax.all_gather(part, axis), array)  19.9 us
    ppermute x1, starting transfers between devices, shifted(): return lax.ppermute(block, axis, route)  16.1 us
    dot_general x1, matrix products, on_device(): jnp.einsum('rk,tk->rt', discount, arrived.reshape(-1, width), preferred_e...  15.1 us
    dot_general x1, matrix products, on_device(): jnp.dot(price, onehot, preferred_element_type=jnp.float32)  13.6 us
  transfers between devices with their start and end apart: 4, of which 3 were waited for; matrix products, arithmetic and copies ran while one was open for 22% of the time, Pallas kernels for 0%

commit v1 on v0

v1 whole, which is shorter than its diff:
```python
import functools

import jax
import jax.numpy as jnp
from jax import lax
from jax.experimental import pallas as pl
from jax.experimental.pallas import tpu as pltpu
from jax.sharding import PartitionSpec as P

MESH = pl.DeviceIdType.MESH
LANES = 128
CHUNKS = 2
F32, BF16 = jnp.float32, jnp.bfloat16


def kernel(
    nd,
    nb,
    shocks,
    persistence,
    volatility,
    base_rate,
    cashflows,
    owner,
    trade_set,
    threshold,
    margin_lag,
    net_out,
    exposure_out,
    flows,
    tile_of,
    outgoing,
    incoming,
    weights,
    factors,
    discount,
    partial,
    arrived,
    packed,
    returned,
    local_sem,
    a_send,
    a_recv,
    b_send,
    b_recv,
    c_send,
    c_recv,
    h_send,
    h_recv,
    e_send,
    e_recv,
    f_send,
    f_recv,
):
    d, o = lax.axis_index("date"), lax.axis_index("book")
    nz = nd // 2
    z, core = d // 2, d % 2
    dates = shocks.shape[0]
    width = shocks.shape[2]
    total_dates = dates * nd
    here = shocks.shape[1] // nd
    piece = here // CHUNKS
    blocks = tile_of.shape[0] - 1
    block_rows = flows.shape[0] // blocks
    set_rows = tile_of.shape[1]
    own_sets = net_out.shape[1]
    column_tiles = width // LANES

    def column_of(index):
        return pl.multiple_of((index % column_tiles) * LANES, LANES)

    def row_of(index):
        return pl.multiple_of((index // column_tiles) * set_rows, set_rows)

    def tile(index):
        return weights.at[pl.ds(row_of(index), set_rows), pl.ds(column_of(index), LANES)]

    barrier = pltpu.get_barrier_semaphore()

    @pl.loop(1, nd)
    def _(i):
        pl.semaphore_signal(barrier, 1, device_id={"date": (d + i) % nd}, device_id_type=MESH)

    @pl.loop(1, nb)
    def _(i):
        pl.semaphore_signal(barrier, 1, device_id={"book": (o + i) % nb}, device_id_type=MESH)

    load = pltpu.make_async_copy(
        cashflows.at[:, pl.ds(column_of(d), LANES)], flows, local_sem.at[CHUNKS]
    )
    load.start()

    def paths_of(q, k):
        return pl.ds(pl.multiple_of(q * here + k * piece, piece), piece)

    def own_factors(k):
        return pltpu.make_async_copy(
            shocks.at[:, paths_of(d, k), :],
            factors.at[k, pl.ds(d * dates, dates)],
            local_sem.at[k],
        )

    for k in range(CHUNKS):
        own_factors(k).start()

    load.wait()
    first_set = (d // column_tiles) * set_rows
    labels = lax.broadcasted_iota(jnp.int32, (set_rows, LANES), 0) + first_set
    rows_each = block_rows // LANES
    for b in range(blocks):
        hot = jnp.concatenate(
            [
                jnp.where(labels == trade_set[b * rows_each + r : b * rows_each + r + 1, :], 1.0, 0.0)
                for r in range(rows_each)
            ],
            axis=1,
        ).astype(BF16)
        tile_of[b] = jnp.dot(
            hot, flows[b * block_rows : (b + 1) * block_rows, :], preferred_element_type=F32
        )
    tile_of[blocks] = jnp.zeros((set_rows, LANES), F32)

    @pl.loop(0, nb)
    def _(target):
        first, second = jnp.int32(blocks), jnp.int32(blocks)
        for b in reversed(range(blocks)):
            named = owner[0, b] == target
            second = jnp.where(named, first, second)
            first = jnp.where(named, b, first)
        outgoing[target] = (tile_of[first] + tile_of[second]).astype(BF16)

    pl.semaphore_wait(barrier, nd + nb - 2)

    def send_factors(i, k):
        q = (d + i) % nd
        return pltpu.make_async_remote_copy(
            src_ref=shocks.at[:, paths_of(q, k), :],
            dst_ref=factors.at[k, pl.ds(d * dates, dates)],
            send_sem=a_send.at[k, q],
            recv_sem=a_recv.at[k, d],
            device_id={"date": q},
            device_id_type=MESH,
        )

    def got_factors(i, k):
        q = (d + i) % nd
        return pltpu.make_async_remote_copy(
            src_ref=shocks.at[:, paths_of(q, k), :],
            dst_ref=factors.at[k, pl.ds(q * dates, dates)],
            send_sem=a_send.at[k, q],
            recv_sem=a_recv.at[k, q],
            device_id={"date": q},
            device_id_type=MESH,
        )

    def send_tile(i):
        q = (o + i) % nb
        return pltpu.make_async_remote_copy(
            src_ref=outgoing.at[q],
            dst_ref=incoming.at[o],
            send_sem=b_send.at[q],
            recv_sem=b_recv.at[o],
            device_id={"book": q},
            device_id_type=MESH,
        )

    def got_tile(i):
        q = (o + i) % nb
        return pltpu.make_async_remote_copy(
            src_ref=outgoing.at[q],
            dst_ref=incoming.at[q],
            send_sem=b_send.at[q],
            recv_sem=b_recv.at[q],
            device_id={"book": q},
            device_id_type=MESH,
        )

    pl.loop(1, nb)(lambda i: send_tile(i).start())
    pl.loop(1, nd)(lambda i: send_factors(i, 0).start())
    pl.loop(1, nb)(lambda i: got_tile(i).wait_recv())

    summed = lax.fori_loop(
        1,
        nb,
        lambda i, total: total + incoming[(o + i) % nb].astype(F32),
        outgoing[o].astype(F32),
    )
    weights[pl.ds(row_of(d), set_rows), pl.ds(column_of(d), LANES)] = summed.astype(BF16)

    def spread(i, sender):
        q = (z + i) % nz
        mine = tile(sender)
        return pltpu.make_async_remote_copy(
            src_ref=mine,
            dst_ref=mine,
            send_sem=c_send.at[q],
            recv_sem=c_recv.at[sender // 2],
            device_id={"date": q * 2 + core},
            device_id_type=MESH,
        )

    def handed(index, from_core):
        at = tile(index * 2 + from_core)
        return pltpu.make_async_remote_copy(
            src_ref=at,
            dst_ref=at,
            send_sem=h_send.at[index],
            recv_sem=h_recv.at[index],
            device_id={"date": d + 1 - 2 * core},
            device_id_type=MESH,
        )

    pl.loop(1, nz)(lambda i: spread(i, d).start())
    handed(z, core).start()
    for k in range(1, CHUNKS):
        pl.loop(1, nd)(lambda i: send_factors(i, k).start())

    keep = persistence[...]
    scale = volatility[...]
    base = base_rate[...]

    def discounts(k):
        own_factors(k).wait()
        pl.loop(1, nd)(lambda i: got_factors(i, k).wait_recv())

        def step(t, level):
            level = keep * level + scale * factors[k, t].astype(F32)
            rows = pl.ds(pl.multiple_of(t * piece, piece), piece)
            discount[rows, :] = jnp.exp(-(base + level)).astype(BF16)
            return level

        lax.fori_loop(0, total_dates, step, jnp.zeros((piece, width), F32), unroll=4)

    def send_partial(i, k):
        q = (o + i) % nb
        return pltpu.make_async_remote_copy(
            src_ref=partial.at[k, pl.ds(pl.multiple_of(q * own_sets, own_sets), own_sets), :],
            dst_ref=arrived.at[k, o],
            send_sem=e_send.at[k, q],
            recv_sem=e_recv.at[k, o],
            device_id={"book": q},
            device_id_type=MESH,
        )

    def got_partial(i, k):
        q = (o + i) % nb
        return pltpu.make_async_remote_copy(
            src_ref=partial.at[k, pl.ds(pl.multiple_of(q * own_sets, own_sets), own_sets), :],
            dst_ref=arrived.at[k, q],
            send_sem=e_send.at[k, q],
            recv_sem=e_recv.at[k, q],
            device_id={"book": q},
            device_id_type=MESH,
        )

    def values(k):
        partial[k] = lax.dot_general(
            weights[...], discount[...], (((1,), (1,)), ((), ())), preferred_element_type=F32
        ).astype(BF16)
        pl.loop(1, nb)(lambda i: send_partial(i, k).start())

    discounts(0)

    @pl.loop(1, nz)
    def _(i):
        q = (z + i) % nz
        spread(i, q * 2 + core).wait_recv()
        handed(q, core).start()

    pl.loop(0, nz)(lambda i: handed(i, 1 - core).wait_recv())
    values(0)
    for k in range(1, CHUNKS):
        discounts(k)
        values(k)

    lane = lax.broadcasted_iota(jnp.int32, (8, LANES), 1)
    groups = LANES // own_sets
    bands = own_sets // 8
    lane_block = lane // own_sets
    lane_piece = lane // piece

    def swapped(tiles):
        out = []
        for m in range(groups):
            made = None
            for a in range(groups):
                shift = ((a - m) * own_sets) % LANES
                moved = pltpu.roll(tiles[a], shift, 1) if shift else tiles[a]
                made = moved if made is None else jnp.where(lane_block == a, moved, made)
            out.append(made)
        return out

    def send_back(i, k):
        q = (d + i) % nd
        depth = 16 if k == CHUNKS - 1 else 8
        return pltpu.make_async_remote_copy(
            src_ref=packed.at[k, q, pl.ds(0, depth), :],
            dst_ref=returned.at[k, d, pl.ds(0, depth), :],
            send_sem=f_send.at[k, q],
            recv_sem=f_recv.at[k, d],
            device_id={"date": q},
            device_id_type=MESH,
        )

    def got_back(i, k):
        q = (d + i) % nd
        depth = 16 if k == CHUNKS - 1 else 8
        return pltpu.make_async_remote_copy(
            src_ref=packed.at[k, q, pl.ds(0, depth), :],
            dst_ref=returned.at[k, q, pl.ds(0, depth), :],
            send_sem=f_send.at[k, q],
            recv_sem=f_recv.at[k, q],
            device_id={"date": q},
            device_id_type=MESH,
        )

    lags = margin_lag[...].reshape(1, 1, own_sets)
    limits = threshold[...].reshape(1, 1, own_sets)
    packed[CHUNKS - 1, :, 8:16, :] = jnp.zeros((nd, 8, LANES), F32)
    exposure = jnp.zeros((total_dates, own_sets), F32)
    for k in range(CHUNKS):
        pl.loop(1, nb)(lambda i: got_partial(i, k).wait_recv())
        own = partial[k, pl.ds(pl.multiple_of(o * own_sets, own_sets), own_sets), :]
        net = lax.fori_loop(
            1,
            nb,
            lambda i, total: total + arrived[k, (o + i) % nb].astype(F32),
            own.astype(F32),
        )
        for g in range(total_dates * piece // LANES):
            tiles = [net[a * 8 : a * 8 + 8, g * LANES : (g + 1) * LANES] for a in range(bands)]
            for m, made in enumerate(swapped(tiles)):
                packed[k, g * groups + m, 0:8, :] = made
        if k < CHUNKS - 1:
            pl.loop(1, nd)(lambda i: send_back(i, k).start())
        by_date = net.T.reshape(total_dates, piece, own_sets)
        zero = jnp.zeros((1, piece, own_sets), F32)
        once = jnp.concatenate([zero, by_date[:-1]], axis=0)
        twice = jnp.concatenate([zero, once[:-1]], axis=0)
        collateral = jnp.where(lags == 1, once, jnp.where(lags == 2, twice, 0.0))
        exposure += jnp.sum(jnp.maximum(by_date - collateral - limits, 0.0), axis=1)
    for q in range(nd):
        packed[CHUNKS - 1, q, 8 : 8 + dates, 0:own_sets] = exposure[q * dates : (q + 1) * dates, :]
    pl.loop(1, nd)(lambda i: send_back(i, CHUNKS - 1).start())

    mean = jnp.zeros((dates, own_sets), F32)
    for k in range(CHUNKS):
        depth = 16 if k == CHUNKS - 1 else 8
        returned[k, d, 0:depth, :] = packed[k, d, 0:depth, :]
        pl.loop(1, nd)(lambda i: got_back(i, k).wait_recv())
        for g in range(nd // groups):
            lanes = slice(g * LANES, (g + 1) * LANES)
            tiles = [returned[k, g * groups + m, 0:8, :] for m in range(groups)]
            for a in range(bands):
                for t in range(dates):
                    rows = slice(a * 8, a * 8 + 8)
                    made = None if k == 0 else net_out[t, rows, lanes]
                    for m in range(groups):
                        shift = (m * here + k * piece - a * own_sets - t * piece) % LANES
                        moved = pltpu.roll(tiles[m], shift, 1) if shift else tiles[m]
                        chosen = lane_piece == m * CHUNKS + k
                        made = moved if made is None else jnp.where(chosen, moved, made)
                    net_out[t, rows, lanes] = made
    for q in range(nd):
        mean += returned[CHUNKS - 1, q, 8 : 8 + dates, 0:own_sets]
    exposure_out[...] = mean * (1.0 / shocks.shape[1])

    for k in range(CHUNKS):
        pl.loop(1, nd)(lambda i: send_factors(i, k).wait_send())
        pl.loop(1, nb)(lambda i: send_partial(i, k).wait_send())
        pl.loop(1, nd)(lambda i: send_back(i, k).wait_send())
    pl.loop(1, nb)(lambda i: send_tile(i).wait_send())
    pl.loop(1, nz)(lambda i: spread(i, d).wait_send())
    pl.loop(0, nz)(lambda i: handed(i, core).wait_send())


def on_device(
    nd,
    nb,
    shocks,
    persistence,
    volatility,
    base_rate,
    cashflows,
    block_owner,
    trade_set,
    threshold,
    margin_lag,
):
    dates, paths, width = shocks.shape
    trades = cashflows.shape[0]
    blocks = block_owner.shape[0]
    own_sets = threshold.shape[0]
    sets = own_sets * nb
    set_rows = sets * width // (nd * LANES)
    here = paths // nd
    piece = here // CHUNKS
    rows = dates * nd * piece
    nz = nd // 2
    vmem = pl.BlockSpec(memory_space=pltpu.VMEM)
    anywhere = pl.BlockSpec(memory_space=pl.ANY)
    dma = pltpu.SemaphoreType.DMA
    net_value, exposure = pl.pallas_call(
        functools.partial(kernel, nd, nb),
        out_shape=(
            jax.ShapeDtypeStruct((dates, own_sets, paths), F32),
            jax.ShapeDtypeStruct((dates, own_sets), F32),
        ),
        in_specs=[
            anywhere,
            vmem,
            vmem,
            vmem,
            anywhere,
            pl.BlockSpec(memory_space=pltpu.SMEM),
            vmem,
            vmem,
            vmem,
        ],
        out_specs=(vmem, vmem),
        scratch_shapes=[
            pltpu.VMEM((trades, LANES), BF16),
            pltpu.VMEM((blocks + 1, set_rows, LANES), F32),
            pltpu.VMEM((nb, set_rows, LANES), BF16),
            pltpu.VMEM((nb, set_rows, LANES), BF16),
            pltpu.VMEM((sets, width), BF16),
            pltpu.VMEM((CHUNKS, dates * nd, piece, width), BF16),
            pltpu.VMEM((rows, width), BF16),
            pltpu.VMEM((CHUNKS, sets, rows), BF16),
            pltpu.VMEM((CHUNKS, nb, own_sets, rows), BF16),
            pltpu.VMEM((CHUNKS, nd, 16, LANES), F32),
            pltpu.VMEM((CHUNKS, nd, 16, LANES), F32),
            dma((CHUNKS + 1,)),
            dma((CHUNKS, nd)),
            dma((CHUNKS, nd)),
            dma((nb,)),
            dma((nb,)),
            dma((nz,)),
            dma((nz,)),
            dma((nz,)),
            dma((nz,)),
            dma((CHUNKS, nb)),
            dma((CHUNKS, nb)),
            dma((CHUNKS, nd)),
            dma((CHUNKS, nd)),
        ],
        compiler_params=pltpu.CompilerParams(collective_id=0, has_side_effects=True),
    )(
        shocks,
        persistence.reshape(1, width),
        volatility.reshape(1, width),
        base_rate.reshape(1, width),
        cashflows,
        block_owner.reshape(1, blocks),
        trade_set.reshape(trades // LANES, LANES),
        threshold.reshape(1, own_sets),
        margin_lag.reshape(1, own_sets),
    )
    return net_value.swapaxes(1, 2), exposure


def solution(mesh):
    return jax.shard_map(
        functools.partial(on_device, mesh.shape["date"], mesh.shape["book"]),
        mesh=mesh,
        in_specs=(
            P("date", None, "book"),
            P("book"),
            P("book"),
            P("book"),
            P("book", None),
            P("book", None),
            P("book"),
            P("book"),
            P("book"),
        ),
        out_specs=(P("date", None, "book"), P("date", "book")),
        check_vma=False,
    )
```

time: 280 us -> 65.8 us (0.23)
  the two profiles are of different devices: /device:TPU:57 before, /device:TPU:1 now
where the time goes in v1:
time: 65.8 us; the launch traced here: 65.6 us
  Pallas kernels  62.2 us (95%)
  local copies, waits for them, and re-layouts  2.8 us (4%)
    pallas_call x1, Pallas kernels, on_device(): pl.pallas_call(functools.partial(kernel, nd, nb), out_shape=(jax.ShapeDty...  62.2 us
    unnamed x2, local copies, waits for them, and re-layouts  2.8 us

profile of v1, /device:TPU:1, one launch (start us, length us, event | category | flops | bytes accessed | tf_op | source)
XLA Modules:
  0.0 65.6 jit_solution(12257621468561606337)
XLA Ops:
  0.6 62.2 %shard_map.104 = (f32[2,32,512]{2,1,0:T(8,128)}, f32[2,32]{1,0:T(2,128)}) custom-call(bf16[2,512,512]{2,1,0:T(8,128)(2,1)} %shocks.1, f32[1,512]{1,0:T(1,128)} %bitcast.10, f32[1,512]{1,0:T(1,128)} %bitcast.11, f32[1,512]{1,0:T(1,128)} %bitcast.12, bf16[4096,512]{1,0:T(8,128)(2,1)} %cashflows.1, s32[1,16]{1,0:T(1,128)} %bitcast.13, s32[32,128]{1,0:T(8,128)} %bitcast.9, ...), custom_call_target="tpu_custom_call" | custom-call | tf_op jit(solution)/shard_map/pallas_call | solution.py:403
  62.8 1.6 %copy.13 = f32[2,512,32]{1,2,0:T(8,128)} copy(f32[2,512,32]{1,2,0:T(8,128)} %bitcast.8) | data formatting | bytes 262144
  64.4 1.2 %copy.14 = f32[2,32]{1,0:T(2,128)} copy(f32[2,32]{1,0:T(2,128)} %get-tuple-element.9) | data formatting | bytes 512

commit v2 on v1

v2 whole, which is shorter than its diff:
```python
import functools

import jax
import jax.numpy as jnp
from jax import lax
from jax.experimental import pallas as pl
from jax.experimental.pallas import tpu as pltpu
from jax.sharding import PartitionSpec as P

MESH = pl.DeviceIdType.MESH
LANES = 128
CHUNKS = 2
PARTS = 2
STEPS = 32700.0
LARGEST = 6.0
F32, BF16 = jnp.float32, jnp.bfloat16


def kernel(
    nd,
    nb,
    shocks,
    persistence,
    volatility,
    base_rate,
    cashflows,
    owner,
    trade_set,
    threshold,
    margin_lag,
    net_out,
    exposure_out,
    flows,
    tile_of,
    outgoing,
    incoming,
    weights,
    lent,
    factors,
    carried,
    gathered,
    prefixes,
    state,
    discount,
    partial,
    arrived,
    net,
    earlier,
    sums,
    sums_got,
    local_sem,
    s_send,
    s_recv,
    a_send,
    a_recv,
    p_send,
    p_recv,
    b_send,
    b_recv,
    c_send,
    c_recv,
    h_send,
    h_recv,
    e_send,
    e_recv,
    l_send,
    l_recv,
    n_send,
    n_recv,
    m_send,
    m_recv,
):
    d, o = lax.axis_index("date"), lax.axis_index("book")
    nz = nd // 2
    z, core = d // 2, d % 2
    other = 1 - core
    dates = shocks.shape[0]
    width = shocks.shape[2]
    span = 2 * dates
    half = shocks.shape[1] // 2
    some = half // CHUNKS
    piece = some // nz
    blocks = tile_of.shape[0] - 1
    block_rows = flows.shape[0] // blocks
    set_rows = tile_of.shape[1]
    part_rows = set_rows // PARTS
    own_sets = net_out.shape[1]
    column_tiles = width // LANES
    partner = {"date": d + 1 - 2 * core}

    def send(src, dst, out_sem, in_sem, where):
        return pltpu.make_async_remote_copy(
            src_ref=src,
            dst_ref=dst,
            send_sem=out_sem,
            recv_sem=in_sem,
            device_id=where,
            device_id_type=MESH,
        )

    def tile(index, h):
        rows = pl.multiple_of((index // column_tiles) * part_rows, part_rows)
        columns = pl.multiple_of((index % column_tiles) * LANES, LANES)
        return h, pl.ds(rows, part_rows), pl.ds(columns, LANES)

    barrier = pltpu.get_barrier_semaphore()

    @pl.loop(1, nd)
    def _(i):
        pl.semaphore_signal(barrier, 1, device_id={"date": (d + i) % nd}, device_id_type=MESH)

    @pl.loop(1, nb)
    def _(i):
        pl.semaphore_signal(barrier, 1, device_id={"book": (o + i) % nb}, device_id_type=MESH)

    columns = pl.ds(pl.multiple_of((d % column_tiles) * LANES, LANES), LANES)
    load = pltpu.make_async_copy(cashflows.at[:, columns], flows, local_sem.at[0])
    load.start()

    def paths_of(c, k):
        return pl.ds(pl.multiple_of(c * half + k * some, some), some)

    mine = pl.ds(core * dates, dates)
    theirs = pl.ds(other * dates, dates)

    def lend(k):
        return pltpu.make_async_copy(
            shocks.at[:, paths_of(other, k), :], lent.at[k], local_sem.at[1 + k]
        )

    def retain(k):
        return pltpu.make_async_copy(
            shocks.at[:, paths_of(core, k), :],
            factors.at[k, mine],
            local_sem.at[1 + CHUNKS + k],
        )

    for k in range(CHUNKS):
        lend(k).start()
        retain(k).start()

    load.wait()
    first_set = (d // column_tiles) * set_rows
    labels = lax.broadcasted_iota(jnp.int32, (set_rows, LANES), 0) + first_set
    rows_each = block_rows // LANES
    for b in range(blocks):
        hot = jnp.concatenate(
            [
                jnp.where(labels == trade_set[b * rows_each + r : b * rows_each + r + 1, :], 1.0, 0.0)
                for r in range(rows_each)
            ],
            axis=1,
        ).astype(BF16)
        tile_of[b] = jnp.dot(
            hot, flows[b * block_rows : (b + 1) * block_rows, :], preferred_element_type=F32
        )
    tile_of[blocks] = jnp.zeros((set_rows, LANES), F32)

    @pl.loop(0, nb)
    def _(target):
        first, second = jnp.int32(blocks), jnp.int32(blocks)
        for b in reversed(range(blocks)):
            named = owner[0, b] == target
            second = jnp.where(named, first, second)
            first = jnp.where(named, b, first)
        outgoing[target] = (tile_of[first] + tile_of[second]).astype(BF16)

    keep = persistence[...]
    scale = volatility[...]
    base = base_rate[...]
    keep_span = keep
    bound_one = 1.0 + keep
    for _ in range(span - 2):
        bound_one = 1.0 + keep * bound_one
    for _ in range(span - 1):
        keep_span = keep_span * keep
    bound_one = bound_one * scale * LARGEST
    to_steps = STEPS / bound_one
    from_steps = bound_one * (1.0 / STEPS)

    for k in range(CHUNKS):
        lend(k).wait()
        retain(k).wait()

    pl.semaphore_wait(barrier, nd + nb - 2)

    def swap_shocks(k, slot):
        return send(lent.at[k], factors.at[k, slot], s_send.at[k], s_recv.at[k], partner)

    def send_tile(i, h):
        q = (o + i) % nb
        rows = pl.ds(h * part_rows, part_rows)
        return send(
            outgoing.at[q, rows], incoming.at[o, rows], b_send.at[h, q], b_recv.at[h, o], {"book": q}
        )

    def got_tile(i, h):
        q = (o + i) % nb
        rows = pl.ds(h * part_rows, part_rows)
        return send(
            outgoing.at[q, rows], incoming.at[q, rows], b_send.at[h, q], b_recv.at[h, q], {"book": q}
        )

    for k in range(CHUNKS):
        swap_shocks(k, mine).start()
    for h in range(PARTS):
        pl.loop(1, nb)(lambda i: send_tile(i, h).start())

    def send_carry(i, k):
        q = (z + i) % nz
        return send(
            carried.at[k, q],
            gathered.at[k, z],
            a_send.at[k, q],
            a_recv.at[k, z],
            {"date": q * 2 + core},
        )

    def got_carry(i, k):
        q = (z + i) % nz
        return send(
            carried.at[k, q],
            gathered.at[k, q],
            a_send.at[k, q],
            a_recv.at[k, q],
            {"date": q * 2 + core},
        )

    for k in range(CHUNKS):
        swap_shocks(k, theirs).wait_recv()

        @pl.loop(0, nz)
        def _(q):
            rows = pl.ds(pl.multiple_of(q * piece, piece), piece)
            total = scale * factors[k, 0, rows, :].astype(F32)
            for t in range(1, span):
                total = keep * total + scale * factors[k, t, rows, :].astype(F32)
            carried[k, q] = jnp.round(total * to_steps).astype(jnp.int32).astype(jnp.int16)

        gathered[k, z] = carried[k, z]
        pl.loop(1, nz)(lambda i: send_carry(i, k).start())

    def spread(i, sender, h):
        q = (z + i) % nz
        at = tile(sender, h)
        return send(
            weights.at[at],
            weights.at[at],
            c_send.at[h, q],
            c_recv.at[h, sender // 2],
            {"date": q * 2 + core},
        )

    def handed(index, from_core, h):
        at = tile(index * 2 + from_core, h)
        return send(weights.at[at], weights.at[at], h_send.at[h, index], h_recv.at[h, index], partner)

    def sum_tiles(h):
        pl.loop(1, nb)(lambda i: got_tile(i, h).wait_recv())
        rows = pl.ds(h * part_rows, part_rows)
        summed = lax.fori_loop(
            1,
            nb,
            lambda i, total: total + incoming[(o + i) % nb, rows, :].astype(F32),
            outgoing[o, rows, :].astype(F32),
        )
        weights[tile(d, h)] = summed.astype(BF16)
        pl.loop(1, nz)(lambda i: spread(i, d, h).start())
        handed(z, core, h).start()

    def send_prefix(i, k):
        q = (z + i) % nz
        return send(
            prefixes.at[k, q], state.at[k, z], p_send.at[k, q], p_recv.at[k, z], {"date": q * 2 + core}
        )

    def got_prefix(i, k):
        q = (z + i) % nz
        return send(
            prefixes.at[k, q], state.at[k, q], p_send.at[k, q], p_recv.at[k, q], {"date": q * 2 + core}
        )

    def prefix(k):
        pl.loop(1, nz)(lambda i: got_carry(i, k).wait_recv())
        level = jnp.zeros((piece, width), F32)
        bound = jnp.zeros_like(bound_one)
        for q in range(nz):
            if q == 0:
                prefixes[k, q] = jnp.zeros((piece, width), jnp.int16)
            else:
                prefixes[k, q] = (
                    jnp.round(level * (STEPS / bound)).astype(jnp.int32).astype(jnp.int16)
                )
            level = keep_span * level + gathered[k, q].astype(F32) * from_steps
            bound = keep_span * bound + bound_one
        state[k, z] = prefixes[k, z]
        pl.loop(1, nz)(lambda i: send_prefix(i, k).start())

    for k in range(max(CHUNKS, PARTS)):
        if k < PARTS:
            sum_tiles(k)
        if k < CHUNKS:
            prefix(k)

    bound_here = jnp.zeros_like(bound_one)
    for q in range(nz - 1):
        bound_here = jnp.where(q < z, keep_span * bound_here + bound_one, bound_here)
    unit = bound_here * (1.0 / STEPS)

    def discounts(k):
        pl.loop(1, nz)(lambda i: got_prefix(i, k).wait_recv())

        @pl.loop(0, nz)
        def _(q):
            rows = pl.ds(pl.multiple_of(q * piece, piece), piece)
            level = state[k, q].astype(F32) * unit
            for t in range(span):
                level = keep * level + scale * factors[k, t, rows, :].astype(F32)
                at = pl.ds(pl.multiple_of(t * some + q * piece, piece), piece)
                discount[k, at, :] = jnp.exp(-(base + level)).astype(BF16)

    def partial_at(q):
        first = q * own_sets
        inside = first % set_rows
        start = (first // set_rows) * part_rows + inside % part_rows
        return inside // part_rows, pl.ds(pl.multiple_of(start, own_sets), own_sets)

    def book_at(h, i):
        each = part_rows // own_sets
        return (i // each) * (set_rows // own_sets) + h * each + i % each

    def send_partial(q, k):
        h, rows = partial_at(q)
        return send(
            partial.at[k, h, rows, :], arrived.at[k, o], e_send.at[k, q], e_recv.at[k, o], {"book": q}
        )

    def got_partial(i, k):
        q = (o + i) % nb
        h, rows = partial_at(q)
        return send(
            partial.at[k, h, rows, :], arrived.at[k, q], e_send.at[k, q], e_recv.at[k, q], {"book": q}
        )

    def values(k, h):
        partial[k, h] = lax.dot_general(
            weights[h], discount[k], (((1,), (1,)), ((), ())), preferred_element_type=F32
        ).astype(BF16)

        @pl.loop(0, nb // PARTS)
        def _(i):
            q = book_at(h, i)

            @pl.when(q != o)
            def _():
                send_partial(q, k).start()

    def forward(h):
        @pl.loop(1, nz)
        def _(i):
            q = (z + i) % nz
            spread(i, q * 2 + core, h).wait_recv()
            handed(q, core, h).start()

    forward(0)
    discounts(0)
    for h in range(PARTS):
        if h:
            forward(h)
        pl.loop(0, nz)(lambda i: handed(i, other, h).wait_recv())
        values(0, h)
    for k in range(1, CHUNKS):
        discounts(k)
        for h in range(PARTS):
            values(k, h)

    def send_earlier(k):
        return send(
            net.at[k, :, pl.ds((span - 2) * some, 2 * some)],
            earlier.at[k],
            l_send.at[k],
            l_recv.at[k],
            {"date": (d + 2) % nd},
        )

    def send_net(k, t, c):
        lanes = pl.ds(pl.multiple_of(((1 - c) * dates + t) * some, some), some)
        return send(
            net.at[k, :, lanes],
            net_out.at[t, :, paths_of(c, k)],
            n_send.at[k, t],
            n_recv.at[k, t],
            partner,
        )

    for k in range(CHUNKS):
        pl.loop(1, nb)(lambda i: got_partial(i, k).wait_recv())
        at, rows = partial_at(o)
        net[k] = lax.fori_loop(
            1,
            nb,
            lambda i, total: total + arrived[k, (o + i) % nb].astype(F32),
            partial[k, at, rows, :].astype(F32),
        )

        @pl.when(z < nz - 1)
        def _():
            send_earlier(k).start()

        for t in range(dates):
            send_net(k, t, core).start()

    lags = jnp.broadcast_to(margin_lag[...], (8, own_sets)).T[:, 0:1]
    limits = jnp.broadcast_to(threshold[...], (8, own_sets)).T[:, 0:1]
    sums[...] = jnp.zeros_like(sums)
    totals = [jnp.zeros((own_sets, some), F32) for _ in range(span)]
    for k in range(CHUNKS):
        for t in range(dates):
            lanes = pl.ds(pl.multiple_of((core * dates + t) * some, some), some)
            net_out[t, :, paths_of(core, k)] = net[k, :, lanes]

        @pl.when(z > 0)
        def _():
            send_earlier(k).wait_recv()

        @pl.when(z == 0)
        def _():
            earlier[k] = jnp.zeros((own_sets, 2 * some), F32)

        known = [earlier[k, :, 0:some], earlier[k, :, some : 2 * some]]
        known += [net[k, :, t * some : (t + 1) * some] for t in range(span)]
        for t in range(span):
            collateral = jnp.where(lags == 1, known[t + 1], jnp.where(lags == 2, known[t], 0.0))
            totals[t] += jnp.maximum(known[t + 2] - collateral - limits, 0.0)
    for t in range(span):
        row = jnp.sum(totals[t].T, axis=0, keepdims=True)
        sums[t // dates, t % dates : t % dates + 1, 0:own_sets] = row

    swap_sums = send(sums.at[other], sums_got, m_send, m_recv, partner)
    swap_sums.start()
    for k in range(CHUNKS):
        for t in range(dates):
            send_net(k, t, other).wait_recv()
    swap_sums.wait_recv()
    both = sums[core, 0:dates, 0:own_sets] + sums_got[0:dates, 0:own_sets]
    exposure_out[...] = both * (1.0 / shocks.shape[1])

    swap_sums.wait_send()
    for k in range(CHUNKS):
        swap_shocks(k, mine).wait_send()
        pl.loop(1, nz)(lambda i: send_carry(i, k).wait_send())
        pl.loop(1, nz)(lambda i: send_prefix(i, k).wait_send())
        pl.loop(1, nb)(lambda i: send_partial((o + i) % nb, k).wait_send())

        @pl.when(z < nz - 1)
        def _():
            send_earlier(k).wait_send()

        for t in range(dates):
            send_net(k, t, core).wait_send()
    for h in range(PARTS):
        pl.loop(1, nb)(lambda i: send_tile(i, h).wait_send())
        pl.loop(1, nz)(lambda i: spread(i, d, h).wait_send())
        pl.loop(0, nz)(lambda i: handed(i, core, h).wait_send())


def on_device(
    nd,
    nb,
    shocks,
    persistence,
    volatility,
    base_rate,
    cashflows,
    block_owner,
    trade_set,
    threshold,
    margin_lag,
):
    dates, paths, width = shocks.shape
    trades = cashflows.shape[0]
    blocks = block_owner.shape[0]
    own_sets = threshold.shape[0]
    sets = own_sets * nb
    set_rows = sets * width // (nd * LANES)
    nz = nd // 2
    some = paths // 2 // CHUNKS
    piece = some // nz
    rows = 2 * dates * some
    vmem = pl.BlockSpec(memory_space=pltpu.VMEM)
    anywhere = pl.BlockSpec(memory_space=pl.ANY)
    dma = pltpu.SemaphoreType.DMA
    net_value, exposure = pl.pallas_call(
        functools.partial(kernel, nd, nb),
        out_shape=(
            jax.ShapeDtypeStruct((dates, own_sets, paths), F32),
            jax.ShapeDtypeStruct((dates, own_sets), F32),
        ),
        in_specs=[
            anywhere,
            vmem,
            vmem,
            vmem,
            anywhere,
            pl.BlockSpec(memory_space=pltpu.SMEM),
            vmem,
            vmem,
            vmem,
        ],
        out_specs=(vmem, vmem),
        scratch_shapes=[
            pltpu.VMEM((trades, LANES), BF16),
            pltpu.VMEM((blocks + 1, set_rows, LANES), F32),
            pltpu.VMEM((nb, set_rows, LANES), BF16),
            pltpu.VMEM((nb, set_rows, LANES), BF16),
            pltpu.VMEM((PARTS, sets // PARTS, width), BF16),
            pltpu.VMEM((CHUNKS, dates, some, width), BF16),
            pltpu.VMEM((CHUNKS, 2 * dates, some, width), BF16),
            pltpu.VMEM((CHUNKS, nz, piece, width), jnp.int16),
            pltpu.VMEM((CHUNKS, nz, piece, width), jnp.int16),
            pltpu.VMEM((CHUNKS, nz, piece, width), jnp.int16),
            pltpu.VMEM((CHUNKS, nz, piece, width), jnp.int16),
            pltpu.VMEM((CHUNKS, rows, width), BF16),
            pltpu.VMEM((CHUNKS, PARTS, sets // PARTS, rows), BF16),
            pltpu.VMEM((CHUNKS, nb, own_sets, rows), BF16),
            pltpu.VMEM((CHUNKS, own_sets, rows), F32),
            pltpu.VMEM((CHUNKS, own_sets, 2 * some), F32),
            pltpu.VMEM((2, 8, LANES), F32),
            pltpu.VMEM((8, LANES), F32),
            dma((1 + 2 * CHUNKS,)),
            dma((CHUNKS,)),
            dma((CHUNKS,)),
            dma((CHUNKS, nz)),
            dma((CHUNKS, nz)),
            dma((CHUNKS, nz)),
            dma((CHUNKS, nz)),
            dma((PARTS, nb)),
            dma((PARTS, nb)),
            dma((PARTS, nz)),
            dma((PARTS, nz)),
            dma((PARTS, nz)),
            dma((PARTS, nz)),
            dma((CHUNKS, nb)),
            dma((CHUNKS, nb)),
            dma((CHUNKS,)),
            dma((CHUNKS,)),
            dma((CHUNKS, dates)),
            dma((CHUNKS, dates)),
            dma,
            dma,
        ],
        compiler_params=pltpu.CompilerParams(collective_id=0, has_side_effects=True),
    )(
        shocks,
        persistence.reshape(1, width),
        volatility.reshape(1, width),
        base_rate.reshape(1, width),
        cashflows,
        block_owner.reshape(1, blocks),
        trade_set.reshape(trades // LANES, LANES),
        threshold.reshape(1, own_sets),
        margin_lag.reshape(1, own_sets),
    )
    return net_value.swapaxes(1, 2), exposure


def solution(mesh):
    return jax.shard_map(
        functools.partial(on_device, mesh.shape["date"], mesh.shape["book"]),
        mesh=mesh,
        in_specs=(
            P("date", None, "book"),
            P("book"),
            P("book"),
            P("book"),
            P("book", None),
            P("book", None),
            P("book"),
            P("book"),
            P("book"),
        ),
        out_specs=(P("date", None, "book"), P("date", "book")),
        check_vma=False,
    )
```

time: 65.8 us -> 56 us (0.85)
  the two profiles are of different devices: /device:TPU:1 before, /device:TPU:57 now
where the time goes in v2:
time: 56 us; the launch traced here: 55.8 us
  Pallas kernels  52.4 us (94%)
  local copies, waits for them, and re-layouts  2.8 us (5%)
  between operations  0.64 us (1%)
    pallas_call x1, Pallas kernels, on_device(): pl.pallas_call(functools.partial(kernel, nd, nb), out_shape=(jax.ShapeDty...  52.4 us
    unnamed x2, local copies, waits for them, and re-layouts  2.8 us

profile of v2, /device:TPU:57, one launch (start us, length us, event | category | flops | bytes accessed | tf_op | source)
XLA Modules:
  0.0 55.8 jit_solution(13244969118494380772)
XLA Ops:
  0.6 52.4 %shard_map.104 = (f32[2,32,512]{2,1,0:T(8,128)}, f32[2,32]{1,0:T(2,128)}) custom-call(bf16[2,512,512]{2,1,0:T(8,128)(2,1)} %shocks.1, f32[1,512]{1,0:T(1,128)} %bitcast.10, f32[1,512]{1,0:T(1,128)} %bitcast.11, f32[1,512]{1,0:T(1,128)} %bitcast.12, bf16[4096,512]{1,0:T(8,128)(2,1)} %cashflows.1, s32[1,16]{1,0:T(1,128)} %bitcast.13, s32[32,128]{1,0:T(8,128)} %bitcast.9, ...), custom_call_target="tpu_custom_call" | custom-call | tf_op jit(solution)/shard_map/pallas_call | solution.py:493
  53.0 1.6 %copy.13 = f32[2,512,32]{1,2,0:T(8,128)} copy(f32[2,512,32]{1,2,0:T(8,128)} %bitcast.8) | data formatting | bytes 262144
  54.6 1.2 %copy.14 = f32[2,32]{1,0:T(2,128)} copy(f32[2,32]{1,0:T(2,128)} %get-tuple-element.9) | data formatting | bytes 512

commit v3 on v2

v3 whole, which is shorter than its diff:
```python
import functools

import jax
import jax.numpy as jnp
from jax import lax
from jax.experimental import pallas as pl
from jax.experimental.pallas import tpu as pltpu
from jax.sharding import PartitionSpec as P

MESH = pl.DeviceIdType.MESH
LANES = 128
CHUNKS = 2
PARTS = 2
SPREADING = (("tiles", 0), ("states", 0), ("tiles", 1), ("states", 1))
PRICING = (
    ("forward", 0),
    ("discounts", 0),
    ("handed", 0),
    ("values", 0, 0),
    ("forward", 1),
    ("handed", 1),
    ("values", 0, 1),
    ("discounts", 1),
    ("values", 1, 0),
    ("values", 1, 1),
)
STEPS = 32700.0
LARGEST = 6.0
F32, BF16 = jnp.float32, jnp.bfloat16


def kernel(
    nd,
    nb,
    shocks,
    keep_hbm,
    scale_hbm,
    base_hbm,
    cashflows,
    owner_hbm,
    sets_hbm,
    limits_hbm,
    lags_hbm,
    net_out,
    exposure_out,
    keep_ref,
    scale_ref,
    base_ref,
    owner,
    trade_set,
    limits_ref,
    lags_ref,
    flows,
    tile_of,
    outgoing,
    incoming,
    weights,
    lent,
    factors,
    carried,
    gathered,
    prefixes,
    state,
    discount,
    partial,
    arrived,
    net,
    other_net,
    earlier,
    local_sem,
    s_send,
    s_recv,
    a_send,
    a_recv,
    p_send,
    p_recv,
    b_send,
    b_recv,
    c_send,
    c_recv,
    h_send,
    h_recv,
    e_send,
    e_recv,
    l_send,
    l_recv,
    n_send,
    n_recv,
):
    d, o = lax.axis_index("date"), lax.axis_index("book")
    nz = nd // 2
    z, core = d // 2, d % 2
    other = 1 - core
    dates = shocks.shape[0]
    width = shocks.shape[2]
    span = 2 * dates
    half = shocks.shape[1] // 2
    some = half // CHUNKS
    piece = some // nz
    blocks = tile_of.shape[0] - 1
    block_rows = flows.shape[0] // blocks
    set_rows = tile_of.shape[1]
    part_rows = set_rows // PARTS
    own_sets = net_out.shape[1]
    column_tiles = width // LANES
    partner = {"date": d + 1 - 2 * core}

    def send(src, dst, out_sem, in_sem, where):
        return pltpu.make_async_remote_copy(
            src_ref=src,
            dst_ref=dst,
            send_sem=out_sem,
            recv_sem=in_sem,
            device_id=where,
            device_id_type=MESH,
        )

    def tile(index, h):
        rows = pl.multiple_of((index // column_tiles) * part_rows, part_rows)
        columns = pl.multiple_of((index % column_tiles) * LANES, LANES)
        return h, pl.ds(rows, part_rows), pl.ds(columns, LANES)

    columns = pl.ds(pl.multiple_of((d % column_tiles) * LANES, LANES), LANES)
    loads = [
        pltpu.make_async_copy(src, dst, local_sem.at[2 * CHUNKS + n])
        for n, (src, dst) in enumerate(
            [
                (cashflows.at[:, columns], flows),
                (sets_hbm, trade_set),
                (owner_hbm, owner),
                (keep_hbm, keep_ref),
                (scale_hbm, scale_ref),
                (base_hbm, base_ref),
                (limits_hbm, limits_ref),
                (lags_hbm, lags_ref),
            ]
        )
    ]
    for load in loads:
        load.start()

    barrier = pltpu.get_barrier_semaphore()

    @pl.loop(1, nd)
    def _(i):
        pl.semaphore_signal(barrier, 1, device_id={"date": (d + i) % nd}, device_id_type=MESH)

    @pl.loop(1, nb)
    def _(i):
        pl.semaphore_signal(barrier, 1, device_id={"book": (o + i) % nb}, device_id_type=MESH)

    def paths_of(c, k):
        return pl.ds(pl.multiple_of(c * half + k * some, some), some)

    mine = pl.ds(core * dates, dates)
    theirs = pl.ds(other * dates, dates)

    def lend(k):
        return pltpu.make_async_copy(
            shocks.at[:, paths_of(other, k), :], lent.at[k], local_sem.at[k]
        )

    def retain(k):
        return pltpu.make_async_copy(
            shocks.at[:, paths_of(core, k), :],
            factors.at[k, mine],
            local_sem.at[CHUNKS + k],
        )

    for k in range(CHUNKS):
        lend(k).start()
        retain(k).start()

    for load in loads:
        load.wait()
    first_set = (d // column_tiles) * set_rows
    row = lax.broadcasted_iota(jnp.int32, (set_rows, LANES), 0)
    spaced = (row % part_rows) // own_sets * PARTS + row // part_rows
    labels = first_set + spaced * own_sets + row % own_sets
    rows_each = block_rows // LANES
    for b in range(blocks):
        hot = jnp.concatenate(
            [
                jnp.where(labels == trade_set[b * rows_each + r : b * rows_each + r + 1, :], 1.0, 0.0)
                for r in range(rows_each)
            ],
            axis=1,
        ).astype(BF16)
        tile_of[b] = jnp.dot(
            hot, flows[b * block_rows : (b + 1) * block_rows, :], preferred_element_type=F32
        )
    tile_of[blocks] = jnp.zeros((set_rows, LANES), F32)

    @pl.loop(0, nb)
    def _(target):
        first, second = jnp.int32(blocks), jnp.int32(blocks)
        for b in reversed(range(blocks)):
            named = owner[0, b] == target
            second = jnp.where(named, first, second)
            first = jnp.where(named, b, first)
        made = (tile_of[first] + tile_of[second]).astype(BF16)
        for h in range(PARTS):
            outgoing[h, target] = made[h * part_rows : (h + 1) * part_rows, :]

    keep = keep_ref[...]
    scale = scale_ref[...]
    base = base_ref[...]
    keep_span = keep
    bound_one = 1.0 + keep
    for _ in range(span - 2):
        bound_one = 1.0 + keep * bound_one
    for _ in range(span - 1):
        keep_span = keep_span * keep
    bound_one = bound_one * scale * LARGEST
    to_steps = STEPS / bound_one
    from_steps = bound_one * (1.0 / STEPS)

    for k in range(CHUNKS):
        lend(k).wait()
        retain(k).wait()

    pl.semaphore_wait(barrier, nd + nb - 2)

    def swap_shocks(k, slot):
        return send(lent.at[k], factors.at[k, slot], s_send, s_recv.at[k], partner)

    def send_tile(i, h):
        q = (o + i) % nb
        return send(outgoing.at[h, q], incoming.at[h, o], b_send.at[h], b_recv.at[h], {"book": q})

    def all_of(src, dst, out_sem, in_sem):
        return send(src, dst, out_sem, in_sem, partner)

    for k in range(CHUNKS):
        swap_shocks(k, mine).start()
    for h in range(PARTS):
        pl.loop(1, nb)(lambda i: send_tile(i, h).start())

    def send_carry(i, k):
        q = (z + i) % nz
        return send(
            carried.at[k, q], gathered.at[k, z], a_send.at[k], a_recv.at[k], {"date": q * 2 + core}
        )

    for k in range(CHUNKS):
        swap_shocks(k, theirs).wait_recv()

        @pl.loop(0, nz)
        def _(q):
            rows = pl.ds(pl.multiple_of(q * piece, piece), piece)
            total = scale * factors[k, 0, rows, :].astype(F32)
            for t in range(1, span):
                total = keep * total + scale * factors[k, t, rows, :].astype(F32)
            carried[k, q] = jnp.round(total * to_steps).astype(jnp.int32).astype(jnp.int16)

        gathered[k, z] = carried[k, z]
        pl.loop(1, nz)(lambda i: send_carry(i, k).start())

    def spread(i, h):
        at = tile(d, h)
        return send(
            weights.at[at],
            weights.at[at],
            c_send.at[h],
            c_recv.at[h],
            {"date": ((z + i) % nz) * 2 + core},
        )

    def handed(index, h):
        at = tile(index * 2 + core, h)
        return send(weights.at[at], weights.at[at], h_send.at[h], h_recv.at[h], partner)

    tile_rows = part_rows * LANES // width

    def tiles(count, h, out_sem, in_sem):
        some_rows = weights.at[h, pl.ds(0, count * tile_rows)]
        return all_of(some_rows, some_rows, out_sem.at[h], in_sem.at[h])

    def got_tiles(h):
        some_tiles = incoming.at[h, pl.ds(0, nb - 1)]
        return all_of(some_tiles, some_tiles, b_send.at[h], b_recv.at[h])

    def sum_tiles(h):
        got_tiles(h).wait_recv()
        summed = lax.fori_loop(
            1,
            nb,
            lambda i, total: total + incoming[h, (o + i) % nb].astype(F32),
            outgoing[h, o].astype(F32),
        )
        weights[tile(d, h)] = summed.astype(BF16)
        pl.loop(1, nz)(lambda i: spread(i, h).start())
        handed(z, h).start()

    def send_prefix(i, k):
        q = (z + i) % nz
        return send(
            prefixes.at[k, q], state.at[k, z], p_send.at[k], p_recv.at[k], {"date": q * 2 + core}
        )

    def slices(src, dst, k, out_sem, in_sem):
        count = pl.ds(0, nz - 1)
        return all_of(src.at[k, count], dst.at[k, count], out_sem.at[k], in_sem.at[k])

    def prefix(k):
        slices(carried, gathered, k, a_send, a_recv).wait_recv()
        level = jnp.zeros((piece, width), F32)
        bound = jnp.zeros_like(bound_one)
        for q in range(nz):
            if q == 0:
                prefixes[k, q] = jnp.zeros((piece, width), jnp.int16)
            else:
                prefixes[k, q] = (
                    jnp.round(level * (STEPS / bound)).astype(jnp.int32).astype(jnp.int16)
                )
            level = keep_span * level + gathered[k, q].astype(F32) * from_steps
            bound = keep_span * bound + bound_one
        state[k, z] = prefixes[k, z]
        pl.loop(1, nz)(lambda i: send_prefix(i, k).start())

    for stage, index in SPREADING:
        (sum_tiles if stage == "tiles" else prefix)(index)

    bound_here = jnp.zeros_like(bound_one)
    for q in range(nz - 1):
        bound_here = jnp.where(q < z, keep_span * bound_here + bound_one, bound_here)
    unit = bound_here * (1.0 / STEPS)

    def discounts(k):
        slices(prefixes, state, k, p_send, p_recv).wait_recv()

        @pl.loop(0, nz)
        def _(q):
            rows = pl.ds(pl.multiple_of(q * piece, piece), piece)
            level = state[k, q].astype(F32) * unit
            for t in range(span):
                level = keep * level + scale * factors[k, t, rows, :].astype(F32)
                at = pl.ds(pl.multiple_of(t * some + q * piece, piece), piece)
                discount[k, at, :] = jnp.exp(-(base + level)).astype(BF16)

    holders = set_rows // own_sets
    each = part_rows // own_sets

    def partial_at(q):
        start = (q // holders) * part_rows + (q % holders) // PARTS * own_sets
        return q % PARTS, pl.ds(pl.multiple_of(start, own_sets), own_sets)

    def book_at(h, i):
        group = (o // holders + i // each) % (nb // holders)
        return group * holders + (o % holders + i) % each * PARTS + h

    def send_partial(q, k):
        h, rows = partial_at(q)
        return send(
            partial.at[k, h, rows, :], arrived.at[k, o], e_send.at[k], e_recv.at[k], {"book": q}
        )

    def partials(k):
        blocks_got = arrived.at[k, pl.ds(0, nb - 1)]
        return all_of(blocks_got, blocks_got, e_send.at[k], e_recv.at[k])

    def values(k, h):
        partial[k, h] = lax.dot_general(
            weights[h], discount[k], (((1,), (1,)), ((), ())), preferred_element_type=F32
        ).astype(BF16)

        @pl.loop(0, nb // PARTS)
        def _(i):
            q = book_at(h, i)

            @pl.when(q != o)
            def _():
                send_partial(q, k).start()

    def forward(h):
        tiles(nz - 1, h, c_send, c_recv).wait_recv()
        pl.loop(1, nz)(lambda i: handed((z + i) % nz, h).start())

    for stage, *index in PRICING:
        if stage == "forward":
            forward(*index)
        elif stage == "handed":
            tiles(nz, index[0], h_send, h_recv).wait_recv()
        elif stage == "discounts":
            discounts(*index)
        else:
            values(*index)

    def send_earlier(k):
        return send(
            net.at[k, :, pl.ds((span - 2) * some, 2 * some)],
            earlier.at[k, core],
            l_send.at[k],
            l_recv.at[k],
            {"date": ((z + 1) % nz) * 2},
        )

    def got_earlier(k):
        return all_of(earlier.at[k], earlier.at[k], l_send.at[k], l_recv.at[k])

    def swap_net(k):
        return send(net.at[k], other_net.at[k], n_send.at[k], n_recv.at[k], partner)

    def receive(k):
        partials(k).wait_recv()
        at, rows = partial_at(o)
        net[k] = lax.fori_loop(
            1,
            nb,
            lambda i, total: total + arrived[k, (o + i) % nb].astype(F32),
            partial[k, at, rows, :].astype(F32),
        )

        @pl.when(z < nz - 1)
        def _():
            send_earlier(k).start()

        swap_net(k).start()

    lags = jnp.broadcast_to(lags_ref[...], (8, own_sets)).T[:, 0:1]
    limits = jnp.broadcast_to(limits_ref[...], (8, own_sets)).T[:, 0:1]
    totals = [jnp.zeros((own_sets, some), F32) for _ in range(dates)]
    now = pl.ds(pl.multiple_of(core * dates * some, dates * some), dates * some)

    def settle(k):
        swap_net(k).wait_recv()

        @pl.when(core == 1)
        def _():
            earlier[k, core] = net[k, :, 0 : 2 * some]
            earlier[k, other] = other_net[k, :, 0 : 2 * some]

        @pl.when((core == 0) & (z == 0))
        def _():
            earlier[k] = jnp.zeros((2, own_sets, 2 * some), F32)

        for ref, side in ((net, core), (other_net, other)):
            values_now = ref[k, :, now]
            for t in range(dates):
                net_out[t, :, paths_of(side, k)] = values_now[:, t * some : (t + 1) * some]

        @pl.when((core == 0) & (z > 0))
        def _():
            got_earlier(k).wait_recv()

        for ref, side in ((net, core), (other_net, other)):
            past, values_now = earlier[k, side], ref[k, :, now]
            known = [past[:, 0:some], past[:, some : 2 * some]]
            known += [values_now[:, t * some : (t + 1) * some] for t in range(dates)]
            for t in range(dates):
                collateral = jnp.where(lags == 1, known[t + 1], jnp.where(lags == 2, known[t], 0.0))
                totals[t] += jnp.maximum(known[t + 2] - collateral - limits, 0.0)

    for k in range(CHUNKS):
        receive(k)
        if k:
            settle(k - 1)
    settle(CHUNKS - 1)
    for t in range(dates):
        row = jnp.sum(totals[t].T, axis=0, keepdims=True)
        exposure_out[t : t + 1, :] = row * (1.0 / shocks.shape[1])

    def finish_sends():
        for k in range(CHUNKS):
            slices(carried, gathered, k, a_send, a_recv).wait_send()
            slices(prefixes, state, k, p_send, p_recv).wait_send()
            partials(k).wait_send()

            @pl.when(z < nz - 1)
            def _():
                send_earlier(k).wait_send()

            swap_net(k).wait_send()
        all_of(lent, lent, s_send, s_recv.at[0]).wait_send()
        for h in range(PARTS):
            tiles(nz - 1, h, c_send, c_recv).wait_send()
            tiles(nz, h, h_send, h_recv).wait_send()
        for h in range(PARTS):
            got_tiles(h).wait_send()

    finish_sends()


def plain(net_ref, exposure_ref, net_out, exposure_out, sems):
    copies = [
        pltpu.make_async_copy(net_ref, net_out, sems.at[0]),
        pltpu.make_async_copy(exposure_ref, exposure_out, sems.at[1]),
    ]
    for copy in copies:
        copy.start()
    for copy in copies:
        copy.wait()


def on_device(
    nd,
    nb,
    shocks,
    persistence,
    volatility,
    base_rate,
    cashflows,
    block_owner,
    trade_set,
    threshold,
    margin_lag,
):
    dates, paths, width = shocks.shape
    trades = cashflows.shape[0]
    blocks = block_owner.shape[0]
    own_sets = threshold.shape[0]
    sets = own_sets * nb
    set_rows = sets * width // (nd * LANES)
    nz = nd // 2
    some = paths // 2 // CHUNKS
    piece = some // nz
    rows = 2 * dates * some
    vmem = pl.BlockSpec(memory_space=pltpu.VMEM)
    anywhere = pl.BlockSpec(memory_space=pl.ANY)
    dma = pltpu.SemaphoreType.DMA
    sent = pl.pallas_call(
        functools.partial(kernel, nd, nb),
        out_shape=(
            pltpu.VMEM((dates, own_sets, paths), F32),
            pltpu.VMEM((dates, own_sets), F32),
        ),
        in_specs=[anywhere] * 9,
        out_specs=(vmem, vmem),
        scratch_shapes=[
            pltpu.VMEM((1, width), F32),
            pltpu.VMEM((1, width), F32),
            pltpu.VMEM((1, width), F32),
            pltpu.SMEM((1, blocks), jnp.int32),
            pltpu.VMEM((trades // LANES, LANES), jnp.int32),
            pltpu.VMEM((1, own_sets), F32),
            pltpu.VMEM((1, own_sets), jnp.int32),
            pltpu.VMEM((trades, LANES), BF16),
            pltpu.VMEM((blocks + 1, set_rows, LANES), F32),
            pltpu.VMEM((PARTS, nb, set_rows // PARTS, LANES), BF16),
            pltpu.VMEM((PARTS, nb, set_rows // PARTS, LANES), BF16),
            pltpu.VMEM((PARTS, sets // PARTS, width), BF16),
            pltpu.VMEM((CHUNKS, dates, some, width), BF16),
            pltpu.VMEM((CHUNKS, 2 * dates, some, width), BF16),
            pltpu.VMEM((CHUNKS, nz, piece, width), jnp.int16),
            pltpu.VMEM((CHUNKS, nz, piece, width), jnp.int16),
            pltpu.VMEM((CHUNKS, nz, piece, width), jnp.int16),
            pltpu.VMEM((CHUNKS, nz, piece, width), jnp.int16),
            pltpu.VMEM((CHUNKS, rows, width), BF16),
            pltpu.VMEM((CHUNKS, PARTS, sets // PARTS, rows), BF16),
            pltpu.VMEM((CHUNKS, nb, own_sets, rows), BF16),
            pltpu.VMEM((CHUNKS, own_sets, rows), F32),
            pltpu.VMEM((CHUNKS, own_sets, rows), F32),
            pltpu.VMEM((CHUNKS, 2, own_sets, 2 * some), F32),
            dma((2 * CHUNKS + 8,)),
            dma,
            dma((CHUNKS,)),
            dma((CHUNKS,)),
            dma((CHUNKS,)),
            dma((CHUNKS,)),
            dma((CHUNKS,)),
            dma((PARTS,)),
            dma((PARTS,)),
            dma((PARTS,)),
            dma((PARTS,)),
            dma((PARTS,)),
            dma((PARTS,)),
            dma((CHUNKS,)),
            dma((CHUNKS,)),
            dma((CHUNKS,)),
            dma((CHUNKS,)),
            dma((CHUNKS,)),
            dma((CHUNKS,)),
        ],
        compiler_params=pltpu.CompilerParams(collective_id=0, has_side_effects=True),
    )(
        shocks,
        persistence.reshape(1, width),
        volatility.reshape(1, width),
        base_rate.reshape(1, width),
        cashflows,
        block_owner.reshape(1, blocks),
        trade_set.reshape(trades // LANES, LANES),
        threshold.reshape(1, own_sets),
        margin_lag.reshape(1, own_sets),
    )
    net_value, exposure = pl.pallas_call(
        plain,
        out_shape=tuple(jax.ShapeDtypeStruct(part.shape, F32) for part in sent),
        in_specs=[vmem, vmem],
        out_specs=(anywhere, anywhere),
        scratch_shapes=[dma((2,))],
    )(*(pltpu.with_memory_space_constraint(part, pltpu.VMEM) for part in sent))
    return net_value.swapaxes(1, 2), exposure


def solution(mesh):
    return jax.shard_map(
        functools.partial(on_device, mesh.shape["date"], mesh.shape["book"]),
        mesh=mesh,
        in_specs=(
            P("date", None, "book"),
            P("book"),
            P("book"),
            P("book"),
            P("book", None),
            P("book", None),
            P("book"),
            P("book"),
            P("book"),
        ),
        out_specs=(P("date", None, "book"), P("date", "book")),
        check_vma=False,
    )
```

time: 56 us -> 47.8 us (0.85)
  the two profiles are of different devices: /device:TPU:57 before, /device:TPU:56 now
where the time goes in v3:
time: 47.8 us; the launch traced here: 47.7 us
  Pallas kernels  47 us (98%)
  between operations  0.64 us (1%)
    pallas_call x1, Pallas kernels, on_device(): pl.pallas_call(functools.partial(kernel, nd, nb), out_shape=(pltpu.VMEM((...  46.4 us

profile of v3, /device:TPU:56, one launch (start us, length us, event | category | flops | bytes accessed | tf_op | source)
XLA Modules:
  0.0 47.7 jit_solution(11716492275429534389)
XLA Ops:
  0.6 46.4 %shard_map.104 = (f32[2,32,512]{2,1,0:T(8,128)S(1)}, f32[2,32]{1,0:T(2,128)S(1)}) custom-call(bf16[2,512,512]{2,1,0:T(8,128)(2,1)} %shocks.1, f32[1,512]{1,0:T(1,128)} %bitcast.9, f32[1,512]{1,0:T(1,128)} %bitcast.10, f32[1,512]{1,0:T(1,128)} %bitcast.11, bf16[4096,512]{1,0:T(8,128)(2,1)} %cashflows.1, s32[1,16]{1,0:T(1,128)} %bitcast.12, ...), custom_call_target="tpu_custom_call" | custom-call | tf_op jit(solution)/shard_map/pallas_call | solution.py:521
  47.0 0.7 %shard_map.105 = (f32[2,32,512]{2,1,0:T(8,128)}, f32[2,32]{1,0:T(2,128)}) custom-call(f32[2,32,512]{2,1,0:T(8,128)S(1)} %get-tuple-element.6.net_ref, f32[2,32]{1,0:T(2,128)S(1)} %get-tuple-element.7.exposure_ref), custom_call_target="tpu_custom_call" | custom-call | tf_op jit(solution)/shard_map/pallas_call | solution.py:586
